TPU v7x, 32 devices: a whole 2x2x4 slice. The times are simulated.
32 devices in a mesh: hi: 16 (over z, x, core), grp: 2 (over y).
Axes of the slice: x: 2, y: 2, z: 4, core: 2. Of those that a mesh axis runs over, the one named last changes fastest.
Arguments:
- rho: float32 [2, 8192, 8192], P(None, ('hi', 'grp')), may hold values from -6 to 9
- perm: int32 [2, 13], replicated, may hold values from 0 to 12, each once within a row
- superop: float32 [2, 2, 16, 16], replicated, may hold values from -0.3 to 1.1
Outputs:
- rho_out: float32 [2, 8192, 8192], P(None, ('hi', 'grp'))
- trace_mean: float32 [], replicated
All inputs are finite; a program needn't handle non-finite values.
Results may differ from a plain program's by a relative error of at most 0.0001.
Values sent between devices are 32-bit elements; how exact they have to be, the bound alone decides.
A program may use at most 384 MiB of HBM per device.

v0:
```python
import functools

import jax
import jax.numpy as jnp
from jax import lax
from jax.experimental import pallas as pl
from jax.experimental.pallas import tpu as pltpu
from jax.sharding import PartitionSpec as P

PAIRS = 2
SPAN = 4**PAIRS
AXES = ("hi", "grp")
VMEM_LIMIT = 60 * 1024 * 1024
LANES = 128
SIDE = 2 * SPAN * SPAN
GROUPS = 2


def relabel_table(order, count):
    return relabel(jnp.arange(count, dtype=jnp.int32), order)


def relabel(positions, order):
    qubits = jnp.arange(order.shape[0], dtype=jnp.int32)[:, None]
    bits = jnp.right_shift(positions[None, :], qubits) & 1
    return jnp.sum(jnp.left_shift(bits, order[:, None]), axis=0)


def gather_body(idx_ref, x_ref, o_ref):
    rows = o_ref.shape[0]
    base = pl.program_id(0) * rows

    @pl.loop(0, rows // 8)
    def _(block):
        start = pl.multiple_of(block * 8, 8)
        for k in range(8):
            src = idx_ref[base + start + k]
            o_ref[pl.ds(start + k, 1), :] = x_ref[pl.ds(src, 1), :]


def gather_rows(x, idx):
    count, width = x.shape
    rows = 512
    return pl.pallas_call(
        gather_body,
        out_shape=jax.ShapeDtypeStruct(x.shape, x.dtype),
        grid_spec=pltpu.PrefetchScalarGridSpec(
            num_scalar_prefetch=1,
            grid=(count // rows,),
            in_specs=[
                pl.BlockSpec((count, width), lambda i, s: (0, 0), pipeline_mode=pl.Buffered(1))
            ],
            out_specs=pl.BlockSpec((rows, width), lambda i, s: (i, 0)),
        ),
        compiler_params=pltpu.CompilerParams(vmem_limit_bytes=VMEM_LIMIT),
        name="gather_rows",
    )(idx, x)


def gather_turn_body(idx_ref, x_ref, o_ref, tmp):
    rows = tmp.shape[0]
    low = pl.program_id(0)

    @pl.loop(0, rows // 8)
    def _(block):
        start = pl.multiple_of(block * 8, 8)
        for k in range(8):
            src = idx_ref[(start + k) * SPAN + low]
            tmp[pl.ds(start + k, 1), :] = x_ref[pl.ds(src, 1), :]

    o_ref[0] = tmp[...].T


def gather_turn(x, idx):
    count, width = x.shape
    rows = count // SPAN
    return pl.pallas_call(
        gather_turn_body,
        out_shape=jax.ShapeDtypeStruct((SPAN, width, rows), x.dtype),
        grid_spec=pltpu.PrefetchScalarGridSpec(
            num_scalar_prefetch=1,
            grid=(SPAN,),
            in_specs=[
                pl.BlockSpec((count, width), lambda i, s: (0, 0), pipeline_mode=pl.Buffered(1))
            ],
            out_specs=pl.BlockSpec((1, width, rows), lambda i, s: (i, 0, 0)),
            scratch_shapes=[pltpu.VMEM((rows, width), x.dtype)],
        ),
        compiler_params=pltpu.CompilerParams(vmem_limit_bytes=VMEM_LIMIT),
        name="gather_turn",
    )(idx, x)


def channel_body(kernel_ref, x_ref, o_ref):
    block = x_ref[...].reshape(2 * SPAN * SPAN, x_ref.shape[-1])
    mixed = jnp.dot(
        kernel_ref[...],
        block,
        precision=lax.Precision.HIGHEST,
        preferred_element_type=jnp.float32,
    )
    o_ref[...] = mixed.reshape(o_ref.shape)


def apply_channel(x, kernel):
    span, width, lanes = x.shape
    blocks = width // (2 * SPAN)
    shaped = x.reshape(span, 2, blocks, SPAN, lanes)
    side = 2 * SPAN * SPAN
    spec = pl.BlockSpec((span, 2, 1, SPAN, lanes), lambda i: (0, 0, i, 0, 0))
    whole = pl.BlockSpec((side, side), lambda i: (0, 0))
    out = pl.pallas_call(
        channel_body,
        out_shape=jax.ShapeDtypeStruct(shaped.shape, x.dtype),
        grid=(blocks,),
        in_specs=[whole, spec],
        out_specs=spec,
        compiler_params=pltpu.CompilerParams(vmem_limit_bytes=VMEM_LIMIT),
        name="channel",
    )(kernel, shaped)
    return out.reshape(x.shape)


def pair_kernel(layer_super):
    real = layer_super[0].reshape(4, 4, 4, 4)
    imag = layer_super[1].reshape(4, 4, 4, 4)

    def outer(a, b):
        both = a[:, None, :, None, :, None, :, None] * b[None, :, None, :, None, :, None, :]
        return both.reshape(SPAN, SPAN, SPAN, SPAN)

    re = outer(real, real) - outer(imag, imag)
    im = outer(real, imag) + outer(imag, real)
    top = jnp.stack([re, -im], axis=2)
    bottom = jnp.stack([im, re], axis=2)
    return jnp.stack([top, bottom], axis=0)


def exchange(x, groups=None):
    return lax.all_to_all(
        x, AXES, split_axis=0, concat_axis=0, tiled=True, axis_index_groups=groups
    )


def swap_local(x, local):
    shaped = x.reshape(x.shape[0] // local, local, 2, local)
    return jnp.transpose(shaped, (0, 3, 2, 1)).reshape(x.shape)


def simple_per_device(rho, perm, superop):
    full = rho.shape[2]
    local = rho.shape[1]
    side = 2 * SPAN * SPAN
    table0 = relabel_table(perm[0], full)
    table1 = relabel_table(perm[1], full)
    kernel0 = jnp.transpose(pair_kernel(superop[0]), (1, 0, 2, 4, 3, 5)).reshape(side, side)
    kernel1 = jnp.transpose(pair_kernel(superop[1]), (2, 0, 1, 5, 3, 4)).reshape(side, side)

    x = rho.reshape(2 * local, full).T
    x = gather_rows(x, table0)
    x = exchange(x)
    x = swap_local(x, local)
    x = gather_turn(x, table0)
    x = apply_channel(x, kernel0)
    x = jnp.transpose(x, (2, 0, 1)).reshape(full, 2 * local)
    x = gather_rows(x, table1)
    x = exchange(x)
    x = swap_local(x, local)
    x = gather_turn(x, table1)
    x = apply_channel(x, kernel1)
    x = jnp.transpose(x, (2, 0, 1)).reshape(full, 2 * local)
    matrix = x.T.reshape(2, local, full)

    return matrix


def params():
    return pltpu.CompilerParams(vmem_limit_bytes=VMEM_LIMIT)


def cost(flops, nbytes):
    return pl.CostEstimate(flops=flops, bytes_accessed=nbytes, transcendentals=0)


def whole():
    return pl.BlockSpec(memory_space=pltpu.VMEM)


def scalars():
    return pl.BlockSpec(memory_space=pltpu.SMEM)


def two_parts(x):
    big = x.astype(jnp.bfloat16)
    return big, (x - big.astype(jnp.float32)).astype(jnp.bfloat16)


def reorder(order, x):
    big, small = two_parts(x)
    y = jnp.dot(order, small, preferred_element_type=jnp.float32)
    return y + jnp.dot(order, big, preferred_element_type=jnp.float32)


def copy_rows(idx_ref, first, step, count, parts, src_ref, dst_ref, base, whole_row=None, skip=0):
    pitch = parts if whole_row is None else whole_row
    near = [idx_ref[step * k] * pitch for k in range(8)]

    @pl.loop(0, count // 16)
    def _(block):
        start = block * 16
        for far in range(0, 16, 8):
            origin = idx_ref[first + step * (start + far)] * pitch + skip
            for k in range(8):
                src = pl.multiple_of(origin + near[k], parts)
                dst = pl.multiple_of((base + start + far + k) * parts, parts)
                dst_ref[pl.ds(dst, parts), :] = src_ref[pl.ds(src, parts), :]


def superop_body(by_row, s_ref, o_ref):
    at = lax.broadcasted_iota(jnp.int32, (SIDE, SPAN), 0)
    entry = lax.broadcasted_iota(jnp.int32, (SIDE, SPAN), 1)
    first, last_ = at // (2 * SPAN), at % SPAN
    row, col = (first, last_) if by_row else (last_, first)

    def spread(pair, values):
        mine = jnp.right_shift(row, 2 * pair) % 4 * 4 + jnp.right_shift(col, 2 * pair) % 4
        pick_ = jnp.where(mine == entry, 1.0, 0.0)
        rows = jnp.dot(
            pick_, values, precision=lax.Precision.HIGHEST, preferred_element_type=jnp.float32
        )
        return lax.dot_general(
            rows,
            pick_,
            (((1,), (1,)), ((), ())),
            precision=lax.Precision.HIGHEST,
            preferred_element_type=jnp.float32,
        )

    re0, im0 = spread(0, s_ref[0]), spread(0, s_ref[1])
    re1, im1 = spread(1, s_ref[0]), spread(1, s_ref[1])
    re = re1 * re0 - im1 * im0
    im = re1 * im0 + im1 * re0
    out_im = lax.broadcasted_iota(jnp.int32, (SIDE, SIDE), 0) // SPAN % 2
    in_im = lax.broadcasted_iota(jnp.int32, (SIDE, SIDE), 1) // SPAN % 2
    o_ref[...] = jnp.where(out_im == in_im, re, jnp.where(out_im == 1, im, -im))


def superop_matrix(layer_super, by_row):
    return pl.pallas_call(
        functools.partial(superop_body, by_row),
        out_shape=jax.ShapeDtypeStruct((SIDE, SIDE), jnp.float32),
        in_specs=[whole()],
        out_specs=whole(),
        compiler_params=params(),
        cost_estimate=cost(10**8, 10**6),
        name="superop",
    )(layer_super)


def turn_body(x_ref, o_ref):
    parts = x_ref.shape[0] // LANES
    cols = x_ref.shape[1]
    for k in range(parts):
        o_ref[pl.ds(k, cols, stride=parts), :] = x_ref[pl.ds(k * LANES, LANES), :].T


def turn_order_body(order_ref, x_ref, o_ref):
    parts = x_ref.shape[0] // LANES
    cols = x_ref.shape[1]
    half = parts // 2
    order = order_ref[...].astype(jnp.bfloat16)
    for part in range(2):
        x = reorder(order, x_ref[pl.ds(part * half * LANES, half * LANES), :])
        for k in range(half):
            o_ref[pl.ds(k * 2 + part, cols, stride=parts), :] = x[k * LANES : (k + 1) * LANES].T


def turn(x, order=None):
    height, full = x.shape
    parts = height // LANES
    cols = 512
    extra = [] if order is None else [order]
    return pl.pallas_call(
        turn_body if order is None else turn_order_body,
        out_shape=jax.ShapeDtypeStruct((full * parts, LANES), x.dtype),
        grid=(full // cols,),
        in_specs=[pl.BlockSpec(o.shape, lambda i: (0, 0)) for o in extra]
        + [pl.BlockSpec((height, cols), lambda i: (0, i))],
        out_specs=pl.BlockSpec((cols * parts, LANES), lambda i: (i, 0)),
        compiler_params=params(),
        cost_estimate=cost(10**8, 2 * x.size * 4),
        name="turn",
    )(*extra, x)


def pick_body(group, share, devices, parts, idx_ref, x_ref, o_ref):
    count = share // GROUPS
    targets = o_ref.shape[0]
    senders = x_ref.shape[0] // (parts * idx_ref.shape[0])
    start = pl.program_id(0) * targets

    @pl.loop(0, targets)
    def _(i):
        d = start + i
        first = d % devices * share + group * count
        skip = d // devices * parts
        copy_rows(idx_ref, first, 1, count, parts, x_ref, o_ref.at[i], 0, senders * parts, skip)


def pick(xt, table, group, devices, parts):
    full = table.shape[0]
    share = full // devices
    targets = devices * (xt.shape[0] // (full * parts))
    steps = 4
    rows = share // GROUPS * parts
    return pl.pallas_call(
        functools.partial(pick_body, group, share, devices, parts),
        out_shape=jax.ShapeDtypeStruct((targets, rows, LANES), xt.dtype),
        grid_spec=pltpu.PrefetchScalarGridSpec(
            num_scalar_prefetch=1,
            grid=(steps,),
            in_specs=[whole()],
            out_specs=pl.BlockSpec((targets // steps, rows, LANES), lambda i, s: (i, 0, 0)),
        ),
        compiler_params=params(),
        cost_estimate=cost(10**8, 3 * xt.size * 4),
        name="pick",
    )(table, xt)


def mix(idx_ref, w_ref, g, xk, tmp):
    high = tmp.shape[0] // 2
    groups = LANES // SPAN

    @pl.loop(0, SPAN)
    def _(low):
        copy_rows(idx_ref, low, SPAN, high, 2, g, tmp, 0)
        for part in range(2):
            turned = tmp[pl.ds(part, high, stride=2), :].T
            at = pl.multiple_of(low * 2 * SPAN + part * SPAN, SPAN)
            xk[:, pl.ds(at, SPAN), :] = turned.reshape(groups, SPAN, high)

    w_big, w_small = two_parts(w_ref[...])

    @pl.loop(0, groups)
    def _(group):
        x_big, x_small = two_parts(xk[group])
        y = jnp.dot(w_big, x_small, preferred_element_type=jnp.float32)
        y += jnp.dot(w_small, x_big, preferred_element_type=jnp.float32)
        y += jnp.dot(w_big, x_big, preferred_element_type=jnp.float32)
        xk[group] = y


def middle_body(chunks, count, blocks, idx_ref, next_ref, w_ref, r_ref, *refs):
    *outs, g, xk, tmp = refs
    sources = r_ref.shape[0]
    parts = r_ref.shape[1] // (LANES * chunks)
    halves = parts // 2
    local = halves * LANES
    high = tmp.shape[0] // 2
    rows = next_ref.shape[0] // (outs[0].shape[0] * blocks)

    @pl.loop(0, chunks)
    def _(c):
        @pl.loop(0, sources)
        def _(s):
            for k in range(parts):
                part, half = k // halves, k % halves
                block = r_ref[s, pl.ds(c * (LANES * parts) + k, LANES, stride=parts), :]
                at = (s * local + half * LANES) * 2 + part
                g[pl.ds(at, LANES, stride=2), :] = block.T

        mix(idx_ref, w_ref, g, xk, tmp)

        @pl.loop(0, SPAN)
        def _(low):
            for part in range(2):
                at = pl.multiple_of(low * 2 * SPAN + part * SPAN, SPAN)
                block = xk[:, pl.ds(at, SPAN), :].reshape(LANES, high)
                g[pl.ds(low * high * 2 + part, high, stride=2), :] = block.T

        @pl.loop(0, outs[0].shape[0])
        def _(d):
            for b in range(blocks):
                out, base = (outs[0], (c * blocks + b) * rows) if count == 1 else (outs[b], c * rows)
                copy_rows(next_ref, (d * blocks + b) * rows, 1, rows, 2, g, out.at[d], base)


def middle(r, table, next_table, w, chunks, devices, blocks, split):
    full = table.shape[0]
    high = full // SPAN
    count = blocks if split else 1
    rows = next_table.shape[0] // (devices * blocks) * chunks * (blocks // count)
    message = jax.ShapeDtypeStruct((devices, 2 * rows, LANES), r.dtype)
    return pl.pallas_call(
        functools.partial(middle_body, chunks, count, blocks),
        out_shape=[message] * count,
        in_specs=[scalars(), scalars(), whole(), whole()],
        out_specs=[whole()] * count,
        scratch_shapes=[
            pltpu.VMEM((full * 2, LANES), r.dtype),
            pltpu.VMEM((LANES // SPAN, SIDE, high), r.dtype),
            pltpu.VMEM((high * 2, LANES), r.dtype),
        ],
        compiler_params=params(),
        cost_estimate=cost(2 * 3 * SIDE * r.size, 2 * r.size * 4),
        name="middle",
    )(table, next_table, w, r)


def last_body(chunks, which, blocks, paired, idx_ref, mine_ref, w_ref, *refs):
    if paired:
        order_ref, *refs = refs
    rs = refs[:GROUPS]
    o_ref, t_ref, g, xk, tmp = refs[-5:]
    full = idx_ref.shape[0]
    high = tmp.shape[0] // 2
    step = pl.program_id(0)
    sources = rs[0].shape[0] // (2 if paired else 1)
    rows = LANES // (2 if paired else 1)
    share = full // sources

    @pl.when(step == 0)
    def _():
        if paired:
            order = order_ref[...].astype(jnp.bfloat16)

        @pl.loop(0, sources)
        def _(s):
            for a, r_ref in enumerate(rs):
                there = blocks if r_ref.shape[1] == 2 * rows * chunks * blocks else 1
                for c in range(chunks):
                    for part in range(2):
                        base = (c * there + (which if there > 1 else 0)) * rows * 2 + part
                        at = pl.ds(base, rows, stride=2)
                        if paired:
                            block = jnp.concatenate([r_ref[s, at, :], r_ref[s + sources, at, :]])
                            block = reorder(order, block)
                        else:
                            block = r_ref[s, at, :]
                        to = (s * share + (a * chunks + c) * LANES) * 2 + part
                        g[pl.ds(to, LANES, stride=2), :] = block.T

        mix(idx_ref, w_ref, g, xk, tmp)

        @pl.loop(0, SPAN)
        def _(low):
            for part in range(2):
                at = pl.multiple_of(low * 2 * SPAN + part * SPAN, SPAN)
                block = xk[:, pl.ds(at, SPAN), :].reshape(LANES, high)
                g[pl.ds(part * full + low, high, stride=SPAN), :] = block.T

    cols = o_ref.shape[2]
    for part in range(2):
        at = pl.multiple_of(part * full + step * cols, LANES)
        o_ref[part] = g[pl.ds(at, cols), :].T

    diagonal = mine_ref[0] + which * LANES

    @pl.when(step == diagonal // cols)
    def _():
        square = o_ref[0, :, pl.ds(pl.multiple_of(diagonal % cols, LANES), LANES)]
        row = lax.broadcasted_iota(jnp.int32, square.shape, 0)
        col = lax.broadcasted_iota(jnp.int32, square.shape, 1)
        mine = jnp.sum(jnp.where(row == col, square, 0.0), axis=0, keepdims=True)
        t_ref[...] = mine + refs[GROUPS][...] if which else mine


def last(rs, table, mine, w, order, chunks, which, blocks, before):
    full = table.shape[0]
    high = full // SPAN
    cols = 1024
    orders = [] if order is None else [order]
    ins = [table, mine, w, *orders, *rs]
    return pl.pallas_call(
        functools.partial(last_body, chunks, which, blocks, order is not None),
        out_shape=(
            jax.ShapeDtypeStruct((2, blocks * LANES, full), rs[0].dtype),
            jax.ShapeDtypeStruct((1, LANES), rs[0].dtype),
        ),
        grid=(full // cols,),
        in_specs=[scalars()] * 2
        + [whole()] * (len(ins) - 2)
        + [whole(), pl.BlockSpec(memory_space=pl.ANY)][: len(before)],
        out_specs=(
            pl.BlockSpec((2, LANES, cols), lambda i: (0, which, i)),
            pl.BlockSpec((1, LANES), lambda i: (0, 0)),
        ),
        scratch_shapes=[
            pltpu.VMEM((full * 2, LANES), rs[0].dtype),
            pltpu.VMEM((LANES // SPAN, SIDE, high), rs[0].dtype),
            pltpu.VMEM((high * 2, LANES), rs[0].dtype),
        ],
        input_output_aliases={len(ins) + 1: 0} if before else {},
        compiler_params=params(),
        cost_estimate=cost(2 * 3 * SIDE * full * 2 * LANES, 4 * full * 2 * LANES * 4),
        name="last",
    )(*ins, *before[::-1])


def sum_over_devices(value, devices):
    return jnp.sum(exchange(jnp.broadcast_to(value, (devices, value.shape[1]))))


def after(x, *done):
    return lax.optimization_barrier((x, *done))[0]


def bit_in(x, at):
    low = jnp.left_shift(1, at) - 1
    return jnp.left_shift(x - (x & low), 1) + (x & low)


def bit_out(x, at):
    low = jnp.left_shift(1, at) - 1
    return jnp.left_shift(jnp.right_shift(x, at + 1), at) + (x & low)


def spread(q, count):
    return q % SPAN * (count // SPAN) + q // SPAN


def run_plan(plan, rho, perm, superop, marks, devices):
    full = rho.shape[2]
    local = full // devices
    blocks = local // LANES
    top = full // 2
    half = devices // 2
    halves = [list(range(half)), list(range(half, devices))]
    table0 = relabel_table(perm[0], full)
    kept, place, final, source = (marks[k] for k in range(4))
    x = rho.reshape(2 * local, full)
    q = jnp.arange(top, dtype=jnp.int32)
    first_groups = second_groups = order = None

    if plan == "full":
        share, parts, chunks = devices, 2 * blocks, 1
        xt = turn(x)
        rows0 = table0
        rows1 = spread(relabel_table(perm[1], full), full)
        targets = devices
    else:
        share, chunks = half, 2
        if plan == "send_keep":
            parts = 2
            at = jnp.arange(local, dtype=jnp.int32)
            new = bit_out(at, source) + (jnp.right_shift(at, source) & 1) * (local // 2)
            xt = turn(x, jnp.where(at[:, None] == new[None, :], 1.0, 0.0))
            old = relabel(bit_in(q, final), perm[0])
            rows0 = old // local * (local // 2) + bit_out(old % local, source)
            stays = final
        else:
            parts = 2 * blocks
            first_groups = halves
            xt = turn(x)
            rows0 = relabel(bit_in(q, kept), perm[0])
            stays = kept
        if plan == "keep_send":
            targets = devices
            few = LANES // 2
            row = q // few * LANES + bit_in(q % few, place)
            at = jnp.arange(LANES, dtype=jnp.int32)
            sent = bit_in(at % few, place) + jnp.left_shift(at // few, place)
            order = jnp.where(at[:, None] == sent[None, :], 1.0, 0.0)
        else:
            targets = half
            second_groups = halves
            row = q
        rows1 = spread(bit_out(relabel(row, perm[1]), stays), top)

    table1 = relabel_table(perm[1], full)
    got = []
    for a in range(GROUPS):
        message = pick(xt, table0, a, share, parts)
        got.append(exchange(after(message, *got[-1:]), first_groups))
    kernel0 = superop_matrix(superop[0], True)
    kernel1 = superop_matrix(superop[1], False)
    done = got[-1]
    parts_of = [[] for _ in range(blocks)]
    for a in range(GROUPS):
        split = a == GROUPS - 1
        messages = middle(got[a], rows0, rows1, kernel0, chunks, targets, blocks, split)
        arrived = []
        for message in messages:
            done = exchange(after(message, done), second_groups)
            arrived.append(done)
        for b in range(blocks):
            parts_of[b].append(arrived[b] if split else arrived[0])
    done = ()
    mine = jnp.reshape(lax.axis_index(AXES).astype(jnp.int32) * local, (1,))
    for b in range(blocks):
        done = last(parts_of[b], table1, mine, kernel1, order, chunks, b, blocks, done)
    return done


def mark_bits(perm):
    qubits = jnp.arange(perm.shape[1], dtype=jnp.int32)
    kept = jnp.sum(jnp.where(perm[0] == qubits[-1], qubits, 0))
    place = jnp.sum(jnp.where(perm[1] == kept, qubits, 0))
    final = perm[1][-1]
    source = jnp.sum(jnp.where(qubits == final, perm[0], 0))
    return jnp.stack([kept, place, final, source])


def choose_plan(marks, local, top_bit):
    low_bits = (SPAN - 1).bit_length()
    kept, place, final, source = (marks[k] for k in range(4))
    plain = kept >= low_bits
    keep_send = plain & (place < LANES.bit_length() - 1)
    keep_keep = plain & (place == top_bit)
    send_keep = (final >= low_bits) & (source < local.bit_length() - 1)
    return jnp.where(keep_send, 1, jnp.where(keep_keep, 2, jnp.where(send_keep, 3, 0)))


def chunked_per_device(rho, perm, superop):
    full = rho.shape[2]
    local = rho.shape[1]
    devices = full // local
    plans = ("full", "keep_send", "keep_keep", "send_keep")
    runs = [functools.partial(run_plan, plan, devices=devices) for plan in plans]
    marks = mark_bits(perm)
    plan = choose_plan(marks, local, perm.shape[1] - 1)
    return lax.switch(plan, runs, rho, perm, superop, marks)


def per_device(rho, perm, superop):
    full = rho.shape[2]
    local = rho.shape[1]
    if local == GROUPS * LANES:
        matrix, diagonal = chunked_per_device(rho, perm, superop)
    else:
        matrix = simple_per_device(rho, perm, superop)
        position = lax.axis_index(AXES)
        block = lax.dynamic_slice_in_dim(matrix[0], position * local, local, 1)
        diagonal = jnp.broadcast_to(jnp.trace(block) / LANES, (1, LANES))
    return (matrix, sum_over_devices(diagonal, full // local) / full)


def solution(mesh):
    assert PAIRS == 2
    placed = (P(None, AXES, None), P(), P())
    return jax.shard_map(
        per_device,
        mesh=mesh,
        in_specs=placed,
        out_specs=(P(None, AXES, None), P()),
        check_vma=False,
    )
```

profile of v0, /device:TPU:0, one launch (start us, length us, event | category | flops | bytes accessed | tf_op | source)
XLA Modules:
  0.0 751.9 jit_solution(2027754584951684055)
XLA Ops:
  0.6 1.3 slice.76
  1.9 0.6 slice.74
  2.5 2.0 fusion.45
  5.9 2.7 fusion.46
  10.4 726.7 %conditional.1 = ((f32[2,256,8192]{2,1,0:T(8,128)}, f32[1,128]{1,0:T(1,128)S(1)})) conditional(s32[]{:T(128)} %clamp.3, (s32[2,13]{1,0:T(2,128)}, f32[2,2,16,16]{3,2,1,0:T(8,128)}, f32[2,256,8192]{2,1,0:T(8,128)}) %tuple.36, (s32[2,13]{1,0:T(2,128)}, f32[2,2,16,16]{3,2,1,0:T(8,128)}, s32[]{:T(128)}, s32[]{:T(128)}, ...), branch_computations={%region_3.6_spmd, %region_6.11_spmd, %region_11.16_spmd, %region_1... | conditional | flops 26271412224 | bytes 333836160 | solution.py:623
  29.5 0.8 slice_bitcast_fusion.14
  30.2 0.8 shift-left_reduce_fusion.10.idx_ref
  31.0 0.7 multiply_add_fusion
  31.6 0.7 fusion.32.order_ref
  32.4 20.5 %turn.7.x_ref = f32[32768,128]{1,0:T(8,128)} custom-call(f32[256,256]{1,0:T(8,128)} %fusion.32.order_ref, f32[512,8192]{1,0:T(8,128)} %bitcast.55), custom_call_target="tpu_custom_call" | custom-call | flops 100000000 | bytes 33554432 | tf_op jit(solution)/shard_map/cond/branch_3_fun/turn/pallas_call | solution.py:283
  52.8 18.5 %pick.14 = f32[32,512,128]{2,1,0:T(8,128)} custom-call(s32[8192]{0:T(1024)} %shift-left_reduce_fusion.10.idx_ref, f32[32768,128]{1,0:T(8,128)} %turn.7.x_ref), custom_call_target="tpu_custom_call" | custom-call | flops 100000000 | bytes 50331648 | tf_op jit(solution)/shard_map/cond/branch_3_fun/pick/pallas_call | solution.py:316
  71.3 7.5 all-to-all-start.15
  78.8 18.6 %pick.15 = f32[32,512,128]{2,1,0:T(8,128)} custom-call(s32[8192]{0:T(1024)} %shift-left_reduce_fusion.10.idx_ref, f32[32768,128]{1,0:T(8,128)} %turn.7.x_ref), custom_call_target="tpu_custom_call" | custom-call | flops 100000000 | bytes 50331648 | tf_op jit(solution)/shard_map/cond/branch_3_fun/pick/pallas_call | solution.py:316
  97.3 0.0 copy-start.3
  97.3 167.5 %all-to-all-done.15.r_ref = f32[32,512,128]{2,1,0:T(8,128)} async-done(((f32[32,512,128]{2,1,0:T(8,128)}), f32[32,512,128]{2,1,0:T(8,128)}, u32[]{:S(2)}, u32[]{:S(2)}) %all-to-all-start.15) | async-done | bytes 8388640 | tf_op jit(solution)/shard_map/cond/branch_3_fun/all_to_all | solution.py:140
  264.9 4.4 all-to-all-start.16
  270.5 0.0 copy-done.3
  270.5 0.6 slice_bitcast_fusion.12
  271.1 7.4 superop.15.w_ref
  278.6 0.2 shift-left_reduce_fusion.12
  278.7 1.3 fusion.34.idx_ref
  280.0 1.3 fusion.36.next_ref
  281.3 51.7 %middle.14 = f32[16,1024,128]{2,1,0:T(8,128)} custom-call(s32[4096]{0:T(1024)} %fusion.34.idx_ref, s32[4096]{0:T(1024)} %fusion.36.next_ref, f32[512,512]{1,0:T(8,128)} %superop.15.w_ref, f32[32,512,128]{2,1,0:T(8,128)} %all-to-all-done.15.r_ref), custom_call_target="tpu_custom_call" | custom-call | flops 6442450944 | bytes 16777216 | tf_op jit(solution)/shard_map/cond/branch_3_fun/middle/pallas_call | solution.py:395
  332.9 122.4 %all-to-all-done.16.r_ref = f32[32,512,128]{2,1,0:T(8,128)} async-done(((f32[32,512,128]{2,1,0:T(8,128)}), f32[32,512,128]{2,1,0:T(8,128)}, u32[]{:S(2)}, u32[]{:S(2)}) %all-to-all-start.16) | async-done | bytes 8388640 | tf_op jit(solution)/shard_map/cond/branch_3_fun/all_to_all | solution.py:140
  455.3 5.3 all-to-all-start.17
  460.7 52.2 %middle.15 = (f32[16,512,128]{2,1,0:T(8,128)}, f32[16,512,128]{2,1,0:T(8,128)}) custom-call(s32[4096]{0:T(1024)} %fusion.34.idx_ref, s32[4096]{0:T(1024)} %fusion.36.next_ref, f32[512,512]{1,0:T(8,128)} %superop.15.w_ref, f32[32,512,128]{2,1,0:T(8,128)} %all-to-all-done.16.r_ref), custom_call_target="tpu_custom_call" | custom-call | flops 6442450944 | bytes 16777216 | tf_op jit(solution)/shard_map/cond/branch_3_fun/middle/pallas_call | solution.py:395
  512.8 65.4 %all-to-all-done.17.refs_0_ = f32[16,1024,128]{2,1,0:T(8,128)} async-done(((f32[16,1024,128]{2,1,0:T(8,128)}), f32[16,1024,128]{2,1,0:T(8,128)}, u32[]{:S(2)}, u32[]{:S(2)}) %all-to-all-start.17) | async-done | bytes 8388640 | tf_op jit(solution)/shard_map/cond/branch_3_fun/all_to_all | solution.py:140
  578.2 54.9 %all_to_all.89.refs_1_ = f32[16,512,128]{2,1,0:T(8,128)} all-to-all(f32[16,512,128]{2,1,0:T(8,128)} %get-tuple-element.79), channel_id=1, replica_groups={{0,1,2,3,4,5,6,7,8,9,10,11,12,13,14,15},{16,17,18,19,20,21,22,23,24,25,..., dimensions={0} | all-to-all | bytes 8388608 | tf_op jit(solution)/shard_map/cond/branch_3_fun/all_to_all | solution.py:140
  633.1 4.9 all-to-all-start.19
  638.0 7.3 superop.14.w_ref
  645.3 0.8 shift-left_reduce_fusion.11.idx_ref
  646.1 41.1 %last.14 = (f32[2,256,8192]{2,1,0:T(8,128)}, f32[1,128]{1,0:T(1,128)}) custom-call(s32[8192]{0:T(1024)} %shift-left_reduce_fusion.11.idx_ref, s32[1]{0:T(128)} %bitcast.19.mine_ref, f32[512,512]{1,0:T(8,128)} %superop.14.w_ref, f32[16,1024,128]{2,1,0:T(8,128)} %all-to-all-done.17.refs_0_, f32[16,512,128]{2,1,0:T(8,128)} %all_to_all.89.refs_1_), custom_call_target="tpu_custom_call" | custom-call | flops 6442450944 | bytes 33554432 | tf_op jit(solution)/shard_map/cond/branch_3_fun/last/pallas_call | solution.py:475
  687.2 9.1 %all-to-all-done.19.refs_1_ = f32[16,512,128]{2,1,0:T(8,128)} async-done(((f32[16,512,128]{2,1,0:T(8,128)}), f32[16,512,128]{2,1,0:T(8,128)}, u32[]{:S(2)}, u32[]{:S(2)}) %all-to-all-start.19) | async-done | bytes 4194336 | tf_op jit(solution)/shard_map/cond/branch_3_fun/all_to_all | solution.py:140
  696.2 40.5 %last.15 = (f32[2,256,8192]{2,1,0:T(8,128)}, f32[1,128]{1,0:T(1,128)S(1)}) custom-call(s32[8192]{0:T(1024)} %shift-left_reduce_fusion.11.idx_ref, s32[1]{0:T(128)} %bitcast.19.mine_ref, f32[512,512]{1,0:T(8,128)} %superop.14.w_ref, f32[16,1024,128]{2,1,0:T(8,128)} %all-to-all-done.17.refs_0_, ...), custom_call_target="tpu_custom_call", output_to_operand_aliasing={{0}: (6, {})} | custom-call | flops 6442450944 | bytes 33554432 | tf_op jit(solution)/shard_map/cond/branch_3_fun/last/pallas_call | solution.py:475
  737.1 11.9 %all_to_all.90 = f32[32,1,128]{2,1,0:T(1,128)S(1)} all-to-all(f32[32,1,128]{2,1,0:T(1,128)S(1)} %broadcast_in_dim.39), channel_id=1, replica_groups=mesh['hi'=16,'grp'=2] {'hi','grp'}, dimensions={0} | all-to-all | bytes 32768 | tf_op jit(solution)/shard_map/all_to_all | solution.py:140
  749.0 0.6 reduce_sum.169
  (3 shorter events, 0.0 us)
Async XLA Ops:
  71.3 193.5 %all-to-all-start.15 = ((f32[32,512,128]{2,1,0:T(8,128)}), f32[32,512,128]{2,1,0:T(8,128)}, u32[]{:S(2)}, u32[]{:S(2)}) async-start(f32[32,512,128]{2,1,0:T(8,128)} %pick.14), calls=%async_computation.15 | async-start | bytes 16777216 | tf_op jit(solution)/shard_map/cond/branch_3_fun/all_to_all | solution.py:140
  97.3 173.2 %copy-start.3 = (f32[2,2,16,16]{3,2,1,0:T(8,128)S(1)}, f32[2,2,16,16]{3,2,1,0:T(8,128)}, u32[]{:S(2)}) copy-start(f32[2,2,16,16]{3,2,1,0:T(8,128)} %get-tuple-element.71) | copy-start | bytes 12292 | tf_op jit(solution)/shard_map/cond
  264.9 190.5 %all-to-all-start.16 = ((f32[32,512,128]{2,1,0:T(8,128)}), f32[32,512,128]{2,1,0:T(8,128)}, u32[]{:S(2)}, u32[]{:S(2)}) async-start(f32[32,512,128]{2,1,0:T(8,128)} %pick.15), calls=%async_computation.16 | async-start | bytes 16777216 | tf_op jit(solution)/shard_map/cond/branch_3_fun/all_to_all | solution.py:140
  455.3 122.9 %all-to-all-start.17 = ((f32[16,1024,128]{2,1,0:T(8,128)}), f32[16,1024,128]{2,1,0:T(8,128)}, u32[]{:S(2)}, u32[]{:S(2)}) async-start(f32[16,1024,128]{2,1,0:T(8,128)} %middle.14), calls=%async_computation.17 | async-start | bytes 16777216 | tf_op jit(solution)/shard_map/cond/branch_3_fun/all_to_all | solution.py:140
  633.1 63.1 %all-to-all-start.19 = ((f32[16,512,128]{2,1,0:T(8,128)}), f32[16,512,128]{2,1,0:T(8,128)}, u32[]{:S(2)}, u32[]{:S(2)}) async-start(f32[16,512,128]{2,1,0:T(8,128)} %get-tuple-element.80), calls=%async_computation.19 | async-start | bytes 8388608 | tf_op jit(solution)/shard_map/cond/branch_3_fun/all_to_all | solution.py:140
where the time goes:
time: 759 us; the launch traced here: 752 us
  waiting for transfers between devices  364 us (48%)
  Pallas kernels  258 us (34%)
  blocking collectives  66.8 us (9%)
  starting transfers between devices  22.1 us (3%)
  loops' own time  20.7 us (3%)
  other arithmetic  11 us (1%)
    all_to_all x4, waiting for transfers between devices, exchange(): lax.all_to_all(x, AXES, split_axis=0, concat_axis=0, tiled=True, axis_ind...  364 us
    pallas_call x2, Pallas kernels, middle(): pl.pallas_call(functools.partial(middle_body, chunks, count, blocks), out...  104 us
    pallas_call x2, Pallas kernels, last(): pl.pallas_call(functools.partial(last_body, chunks, which, blocks, order...  81.6 us
    all_to_all x2, blocking collectives, exchange(): lax.all_to_all(x, AXES, split_axis=0, concat_axis=0, tiled=True, axis_ind...  66.8 us
    pallas_call x2, Pallas kernels, pick(): pl.pallas_call(functools.partial(pick_body, group, share, devices, parts)...  37 us
    all_to_all x4, starting transfers between devices, exchange(): lax.all_to_all(x, AXES, split_axis=0, concat_axis=0, tiled=True, axis_ind...  22.1 us
    another operation x1, loops' own time, chunked_per_device(): return lax.switch(plan, runs, rho, perm, superop, marks)  20.7 us
    pallas_call x1, Pallas kernels, turn(): pl.pallas_call(turn_body if order is None else turn_order_body, out_shape...  20.5 us
  transfers between devices with their start and end apart: 4, of which 4 were waited for; matrix products, arithmetic and copies ran while one was open for 1% of the time, Pallas kernels for 24%

commit v1 on v0

--- a/solution.py
+++ b/solution.py
@@ -293,34 +293,33 @@
     )(*extra, x)
 
 
-def pick_body(group, share, devices, parts, idx_ref, x_ref, o_ref):
+def pick_body(groups, share, devices, parts, idx_ref, x_ref, *outs):
     count = share // GROUPS
-    targets = o_ref.shape[0]
+    targets = outs[0].shape[0]
     senders = x_ref.shape[0] // (parts * idx_ref.shape[0])
     start = pl.program_id(0) * targets
 
     @pl.loop(0, targets)
     def _(i):
         d = start + i
-        first = d % devices * share + group * count
         skip = d // devices * parts
-        copy_rows(idx_ref, first, 1, count, parts, x_ref, o_ref.at[i], 0, senders * parts, skip)
-
-
-def pick(xt, table, group, devices, parts):
+        for group, out in zip(groups, outs):
+            first = d % devices * share + group * count
+            copy_rows(idx_ref, first, 1, count, parts, x_ref, out.at[i], 0, senders * parts, skip)
+
+
+def pick(xt, table, groups, devices, parts):
     full = table.shape[0]
     share = full // devices
     targets = devices * (xt.shape[0] // (full * parts))
     steps = 4
     rows = share // GROUPS * parts
+    spec = pl.BlockSpec((targets // steps, rows, LANES), lambda i, s: (i, 0, 0))
     return pl.pallas_call(
-        functools.partial(pick_body, group, share, devices, parts),
-        out_shape=jax.ShapeDtypeStruct((targets, rows, LANES), xt.dtype),
+        functools.partial(pick_body, groups, share, devices, parts),
+        out_shape=[jax.ShapeDtypeStruct((targets, rows, LANES), xt.dtype)] * len(groups),
         grid_spec=pltpu.PrefetchScalarGridSpec(
-            num_scalar_prefetch=1,
-            grid=(steps,),
-            in_specs=[whole()],
-            out_specs=pl.BlockSpec((targets // steps, rows, LANES), lambda i, s: (i, 0, 0)),
+            num_scalar_prefetch=1, grid=(steps,), in_specs=[whole()], out_specs=[spec] * len(groups)
         ),
         compiler_params=params(),
         cost_estimate=cost(10**8, 3 * xt.size * 4),
@@ -560,8 +559,8 @@
             few = LANES // 2
             row = q // few * LANES + bit_in(q % few, place)
             at = jnp.arange(LANES, dtype=jnp.int32)
-            sent = bit_in(at % few, place) + jnp.left_shift(at // few, place)
-            order = jnp.where(at[:, None] == sent[None, :], 1.0, 0.0)
+            from_two = bit_in(at % few, place) + jnp.left_shift(at // few, place)
+            order = jnp.where(at[:, None] == from_two[None, :], 1.0, 0.0)
         else:
             targets = half
             second_groups = halves
@@ -570,9 +569,14 @@
 
     table1 = relabel_table(perm[1], full)
     got = []
-    for a in range(GROUPS):
-        message = pick(xt, table0, a, share, parts)
-        got.append(exchange(after(message, *got[-1:]), first_groups))
+    if first_groups is None:
+        sent = [pick(xt, table0, (a,), share, parts)[0] for a in range(GROUPS)]
+        got.append(exchange(sent[0]))
+    else:
+        sent = pick(xt, table0, tuple(range(GROUPS)), share, parts)
+        got.append(exchange(after(*sent), first_groups))
+    for message in sent[1:]:
+        got.append(exchange(after(message, got[-1]), first_groups))
     kernel0 = superop_matrix(superop[0], True)
     kernel1 = superop_matrix(superop[1], False)
     done = got[-1]
@@ -609,14 +613,14 @@
     keep_send = plain & (place < LANES.bit_length() - 1)
     keep_keep = plain & (place == top_bit)
     send_keep = (final >= low_bits) & (source < local.bit_length() - 1)
-    return jnp.where(keep_send, 1, jnp.where(keep_keep, 2, jnp.where(send_keep, 3, 0)))
+    return jnp.where(keep_send, 3, jnp.where(keep_keep, 0, jnp.where(send_keep, 1, 2)))
 
 
 def chunked_per_device(rho, perm, superop):
     full = rho.shape[2]
     local = rho.shape[1]
     devices = full // local
-    plans = ("full", "keep_send", "keep_keep", "send_keep")
+    plans = ("keep_keep", "send_keep", "full", "keep_send")
     runs = [functools.partial(run_plan, plan, devices=devices) for plan in plans]
     marks = mark_bits(perm)
     plan = choose_plan(marks, local, perm.shape[1] - 1)

time: 759 us -> 739 us (0.974)
  blocking collectives: 66.8 us -> 210 us
  waiting for transfers between devices: 364 us -> 233 us
  Pallas kernels: 258 us -> 240 us
  loops' own time: 20.7 us -> 8.54 us
    all_to_all x2 -> x3, blocking collectives: 66.8 us -> 210 us  [exchange(): lax.all_to_all(x, AXES, split_axis=0, concat_axis=0, tiled=True, axis_ind...]
    all_to_all x4 -> x3, waiting for transfers between devices: 364 us -> 233 us  [exchange(): lax.all_to_all(x, AXES, split_axis=0, concat_axis=0, tiled=True, axis_ind...]
    pallas_call x2 -> x1, Pallas kernels: 37 us -> 19.7 us  [pick(): pl.pallas_call(functools.partial(pick_body, groups, share, devices, parts...]
    another operation x1, loops' own time: 20.7 us -> 8.54 us  [chunked_per_device(): return lax.switch(plan, runs, rho, perm, superop, marks)]
    all_to_all x4 -> x3, starting transfers between devices: 22.1 us -> 15.6 us  [exchange(): lax.all_to_all(x, AXES, split_axis=0, concat_axis=0, tiled=True, axis_ind...]
  transfers between devices with their start and end apart: 4 -> 3, of which waited for: 4 -> 3; matrix products, arithmetic and copies ran while one was open for 1% -> 1% of each run, Pallas kernels for 24% -> 22%
where the time goes in v1:
time: 739 us; the launch traced here: 726 us
  Pallas kernels  240 us (32%)
  waiting for transfers between devices  233 us (32%)
  blocking collectives  210 us (28%)
  starting transfers between devices  15.6 us (2%)
  other arithmetic  10.3 us (1%)
  loops' own time  8.54 us (1%)
    all_to_all x3, waiting for transfers between devices, exchange(): lax.all_to_all(x, AXES, split_axis=0, concat_axis=0, tiled=True, axis_ind...  233 us
    all_to_all x3, blocking collectives, exchange(): lax.all_to_all(x, AXES, split_axis=0, concat_axis=0, tiled=True, axis_ind...  210 us
    pallas_call x2, Pallas kernels, middle(): pl.pallas_call(functools.partial(middle_body, chunks, count, blocks), out...  99.7 us
    pallas_call x2, Pallas kernels, last(): pl.pallas_call(functools.partial(last_body, chunks, which, blocks, order...  87 us
    pallas_call x1, Pallas kernels, pick(): pl.pallas_call(functools.partial(pick_body, groups, share, devices, parts...  19.7 us
    pallas_call x1, Pallas kernels, turn(): pl.pallas_call(turn_body if order is None else turn_order_body, out_shape...  19.2 us
    all_to_all x3, starting transfers between devices, exchange(): lax.all_to_all(x, AXES, split_axis=0, concat_axis=0, tiled=True, axis_ind...  15.6 us
  transfers between devices with their start and end apart: 3, of which 3 were waited for; matrix products, arithmetic and copies ran while one was open for 1% of the time, Pallas kernels for 22%

profile of v1, /device:TPU:0, one launch (start us, length us, event | category | flops | bytes accessed | tf_op | source)
XLA Modules:
  0.0 726.1 jit_solution(18017096804402292602)
XLA Ops:
  0.6 1.3 slice.76
  1.9 0.6 slice.74
  2.5 2.0 fusion.45
  5.8 2.7 fusion.46
  10.6 702.2 %conditional.1 = ((f32[2,256,8192]{2,1,0:T(8,128)}, f32[1,128]{1,0:T(1,128)S(1)})) conditional(s32[]{:T(128)} %clamp.3, (s32[2,13]{1,0:T(2,128)}, f32[2,2,16,16]{3,2,1,0:T(8,128)}, s32[]{:T(128)}, f32[2,256,8192]{2,1,0:T(8,128)}) %tuple.38, (s32[2,13]{1,0:T(2,128)}, f32[2,2,16,16]{3,2,1,0:T(8,128)}, ...), branch_computations={%region_3.8_spmd, %region_8.13_spmd, %region_13.16_spmd, %region_1... | conditional | flops 26271412224 | bytes 333836160 | solution.py:627
  16.9 0.8 slice_bitcast_fusion.14
  17.6 0.8 shift-left_reduce_fusion.10.idx_ref
  18.4 19.2 %turn.7.x_ref = f32[32768,128]{1,0:T(8,128)} custom-call(f32[512,8192]{1,0:T(8,128)} %bitcast.55), custom_call_target="tpu_custom_call" | custom-call | flops 100000000 | bytes 33554432 | tf_op jit(solution)/shard_map/cond/branch_3_fun/turn/pallas_call | solution.py:283
  37.6 19.7 %pick.11 = (f32[16,1024,128]{2,1,0:T(8,128)}, f32[16,1024,128]{2,1,0:T(8,128)}) custom-call(s32[8192]{0:T(1024)} %shift-left_reduce_fusion.10.idx_ref, f32[32768,128]{1,0:T(8,128)} %turn.7.x_ref), custom_call_target="tpu_custom_call" | custom-call | flops 100000000 | bytes 50331648 | tf_op jit(solution)/shard_map/cond/branch_3_fun/pick/pallas_call | solution.py:318
  57.3 100.9 %all_to_all.90.r_ref = f32[16,1024,128]{2,1,0:T(8,128)} all-to-all(f32[16,1024,128]{2,1,0:T(8,128)} %get-tuple-element.79), channel_id=1, replica_groups={{0,1,2,3,4,5,6,7,8,9,10,11,12,13,14,15},{16,17,18,19,20,21,22,23,24,25,..., dimensions={0} | all-to-all | bytes 16777216 | tf_op jit(solution)/shard_map/cond/branch_3_fun/all_to_all | solution.py:140
  158.2 0.0 copy-start.3
  158.2 4.9 all-to-all-start.16
  165.1 0.0 copy-done.3
  165.1 0.6 slice_bitcast_fusion.12
  165.7 7.4 %superop.15.w_ref = f32[512,512]{1,0:T(8,128)} custom-call(f32[2,16,16]{2,1,0:T(8,128)} %get-tuple-element.114.s_ref), custom_call_target="tpu_custom_call" | custom-call | flops 100000000 | bytes 1000000 | tf_op jit(solution)/shard_map/cond/branch_3_fun/superop/pallas_call | solution.py:249
  173.1 0.8 shift-left_reduce_fusion.12
  173.9 1.2 fusion.36.next_ref
  175.2 49.5 %middle.14 = f32[32,512,128]{2,1,0:T(8,128)} custom-call(s32[4096]{0:T(1024)} %get-tuple-element.119.idx_ref, s32[4096]{0:T(1024)} %fusion.36.next_ref, f32[512,512]{1,0:T(8,128)} %superop.15.w_ref, f32[16,1024,128]{2,1,0:T(8,128)} %all_to_all.90.r_ref), custom_call_target="tpu_custom_call" | custom-call | flops 6442450944 | bytes 16777216 | tf_op jit(solution)/shard_map/cond/branch_3_fun/middle/pallas_call | solution.py:394
  224.7 55.7 %all-to-all-done.16.r_ref = f32[16,1024,128]{2,1,0:T(8,128)} async-done(((f32[16,1024,128]{2,1,0:T(8,128)}), f32[16,1024,128]{2,1,0:T(8,128)}, u32[]{:S(2)}, u32[]{:S(2)}) %all-to-all-start.16) | async-done | bytes 8388640 | tf_op jit(solution)/shard_map/cond/branch_3_fun/all_to_all | solution.py:140
  280.4 6.7 all-to-all-start.17
  287.1 50.2 %middle.15 = (f32[32,256,128]{2,1,0:T(8,128)}, f32[32,256,128]{2,1,0:T(8,128)}) custom-call(s32[4096]{0:T(1024)} %get-tuple-element.119.idx_ref, s32[4096]{0:T(1024)} %fusion.36.next_ref, f32[512,512]{1,0:T(8,128)} %superop.15.w_ref, f32[16,1024,128]{2,1,0:T(8,128)} %all-to-all-done.16.r_ref), custom_call_target="tpu_custom_call" | custom-call | flops 6442450944 | bytes 16777216 | tf_op jit(solution)/shard_map/cond/branch_3_fun/middle/pallas_call | solution.py:394
  337.3 135.9 %all-to-all-done.17.refs_1_ = f32[32,512,128]{2,1,0:T(8,128)} async-done(((f32[32,512,128]{2,1,0:T(8,128)}), f32[32,512,128]{2,1,0:T(8,128)}, u32[]{:S(2)}, u32[]{:S(2)}) %all-to-all-start.17) | async-done | bytes 8388640 | tf_op jit(solution)/shard_map/cond/branch_3_fun/all_to_all | solution.py:140
  473.1 98.0 %all_to_all.91.refs_2_ = f32[32,256,128]{2,1,0:T(8,128)} all-to-all(f32[32,256,128]{2,1,0:T(8,128)} %get-tuple-element.85), channel_id=1, replica_groups=mesh['hi'=16,'grp'=2] {'hi','grp'}, dimensions={0} | all-to-all | bytes 8388608 | tf_op jit(solution)/shard_map/cond/branch_3_fun/all_to_all | solution.py:140
  571.1 4.0 all-to-all-start.19
  575.2 7.3 %superop.14.w_ref = f32[512,512]{1,0:T(8,128)} custom-call(f32[2,16,16]{2,1,0:T(8,128)} %get-tuple-element.115.s_ref), custom_call_target="tpu_custom_call" | custom-call | flops 100000000 | bytes 1000000 | tf_op jit(solution)/shard_map/cond/branch_3_fun/superop/pallas_call | solution.py:249
  582.5 0.7 fusion.43
  583.2 0.8 shift-left_reduce_fusion.11.idx_ref
  583.9 0.6 fusion.25.refs_0_
  584.6 43.4 %last.14 = (f32[2,256,8192]{2,1,0:T(8,128)}, f32[1,128]{1,0:T(1,128)}) custom-call(s32[8192]{0:T(1024)} %shift-left_reduce_fusion.11.idx_ref, s32[1]{0:T(128)} %bitcast.20.mine_ref, f32[512,512]{1,0:T(8,128)} %superop.14.w_ref, f32[128,128]{1,0:T(8,128)} %fusion.25.refs_0_, f32[32,512,128]{2,1,0:T(8,128)} %all-to-all-done.17.refs_1_, ...), custom_call_target="tpu_custom_call" | custom-call | flops 6442450944 | bytes 33554432 | tf_op jit(solution)/shard_map/cond/branch_3_fun/last/pallas_call | solution.py:474
  628.0 41.0 %all-to-all-done.19.refs_2_ = f32[32,256,128]{2,1,0:T(8,128)} async-done(((f32[32,256,128]{2,1,0:T(8,128)}), f32[32,256,128]{2,1,0:T(8,128)}, u32[]{:S(2)}, u32[]{:S(2)}) %all-to-all-start.19) | async-done | bytes 4194336 | tf_op jit(solution)/shard_map/cond/branch_3_fun/all_to_all | solution.py:140
  669.0 43.5 %last.15 = (f32[2,256,8192]{2,1,0:T(8,128)}, f32[1,128]{1,0:T(1,128)S(1)}) custom-call(s32[8192]{0:T(1024)} %shift-left_reduce_fusion.11.idx_ref, s32[1]{0:T(128)} %bitcast.20.mine_ref, f32[512,512]{1,0:T(8,128)} %superop.14.w_ref, f32[128,128]{1,0:T(8,128)} %fusion.25.refs_0_, ...), custom_call_target="tpu_custom_call", output_to_operand_aliasing={{0}: (7, {})} | custom-call | flops 6442450944 | bytes 33554432 | tf_op jit(solution)/shard_map/cond/branch_3_fun/last/pallas_call | solution.py:474
  712.8 10.7 %all_to_all.92 = f32[32,1,128]{2,1,0:T(1,128)S(1)} all-to-all(f32[32,1,128]{2,1,0:T(1,128)S(1)} %broadcast_in_dim.31), channel_id=1, replica_groups=mesh['hi'=16,'grp'=2] {'hi','grp'}, dimensions={0} | all-to-all | bytes 32768 | tf_op jit(solution)/shard_map/all_to_all | solution.py:140
  723.5 0.6 reduce_sum.169
  (4 shorter events, 0.0 us)
Async XLA Ops:
  158.2 6.9 copy-start.3
  158.2 122.2 %all-to-all-start.16 = ((f32[16,1024,128]{2,1,0:T(8,128)}), f32[16,1024,128]{2,1,0:T(8,128)}, u32[]{:S(2)}, u32[]{:S(2)}) async-start(f32[16,1024,128]{2,1,0:T(8,128)} %get-tuple-element.81), calls=%async_computation.16 | async-start | bytes 16777216 | tf_op jit(solution)/shard_map/cond/branch_3_fun/all_to_all | solution.py:140
  280.4 192.7 %all-to-all-start.17 = ((f32[32,512,128]{2,1,0:T(8,128)}), f32[32,512,128]{2,1,0:T(8,128)}, u32[]{:S(2)}, u32[]{:S(2)}) async-start(f32[32,512,128]{2,1,0:T(8,128)} %middle.14), calls=%async_computation.17 | async-start | bytes 16777216 | tf_op jit(solution)/shard_map/cond/branch_3_fun/all_to_all | solution.py:140
  571.1 97.9 %all-to-all-start.19 = ((f32[32,256,128]{2,1,0:T(8,128)}), f32[32,256,128]{2,1,0:T(8,128)}, u32[]{:S(2)}, u32[]{:S(2)}) async-start(f32[32,256,128]{2,1,0:T(8,128)} %get-tuple-element.86), calls=%async_computation.19 | async-start | bytes 8388608 | tf_op jit(solution)/shard_map/cond/branch_3_fun/all_to_all | solution.py:140
